TPU v7x, 32 devices: a whole 2x2x4 slice. The times are simulated.
32 devices in a mesh: tab: 8 (over z, x), rep: 4 (over y, core).
Axes of the slice: x: 2, y: 2, z: 4, core: 2. Of those that a mesh axis runs over, the one named last changes fastest.
Arguments:
- sample_ids: int32 [16384, 26], P(('tab', 'rep')), may hold values from 0 to 4095, as said below
- features: bfloat16 [16384, 27, 128], P(('tab', 'rep')), may hold values from -6 to 6
- pair_grad: bfloat16 [351, 16384], P(None, ('tab', 'rep')), may hold values from -1.59375 to 1.59375
Outputs:
- table_grad: float32 [26, 4096, 128], P(None, ('tab', 'rep'))
- dense_grad: float32 [16384, 128], P(('tab', 'rep'))
Inputs may be any that keep to these rules, and one draw needn't show every extreme that they name: `sample_ids`: row r is owned by device r // 128, numbered tab * 4 + rep. For each field and the 512 samples of one device (aligned blocks of rows in device order), at most 32 ids fall in the rows of any one device, and at most 128 in the rows of any one tab index; in every block and field both bounds are reached.
All inputs are finite; a program needn't handle non-finite values.
Results may differ from a plain program's by a relative error of at most 0.0029.
Values may be sent and summed in bfloat16 or wider, within the bound.
No kernel may reach another device: no remote copies, remote signals or barrier semaphores. Data moves between devices by JAX's collectives and lax.ppermute only.
A program may use at most 128 MiB of HBM per device.

v0:
```python
import jax
import jax.numpy as jnp
import numpy as np
from jax import lax
from jax.sharding import PartitionSpec as P

RQ = 128


def pair_table(vectors):
    row_of, col_of = np.tril_indices(vectors, -1)
    spread = np.zeros((row_of.shape[0], vectors * vectors), np.float32)
    places = np.arange(row_of.shape[0])
    spread[places, row_of * vectors + col_of] = 1.0
    spread[places, col_of * vectors + row_of] = 1.0
    return spread


def arrival_order(targets, bins):
    matches = (targets[:, None] == jnp.arange(bins, dtype=jnp.int32)[None, :]).astype(jnp.int32)
    return jnp.sum(jnp.cumsum(matches, axis=0) * matches, axis=1) - 1


def place_field(slot_of, tag_of, grads, slot_total):
    placing = jnp.arange(slot_total, dtype=jnp.int32)[:, None] == slot_of[None, :]
    placed = jnp.dot(
        placing.astype(jnp.bfloat16), grads, preferred_element_type=jnp.float32
    ).astype(jnp.bfloat16)
    shifted = (tag_of + 1).astype(jnp.float32)
    tag_sum = jnp.dot(placing.astype(jnp.float32), shifted, precision=lax.Precision.HIGHEST)
    return (placed, tag_sum.astype(jnp.int32) - 1)


def tally_rows(arrived, row_tags, row_count):

    def per_field(pieces):
        slot_grads, slot_tags = pieces
        matches = (slot_tags[None, :] == jnp.arange(row_count, dtype=jnp.int32)[:, None]).astype(
            jnp.bfloat16
        )
        return jnp.dot(matches, slot_grads, preferred_element_type=jnp.float32)

    return lax.map(per_field, (arrived, row_tags))


def local(sample_ids, features, pair_grad):
    vectors = features.shape[1]
    samples = features.shape[0]
    depth = features.shape[2]
    spread = jnp.asarray(pair_table(vectors).T).astype(jnp.bfloat16)
    symmetric = jnp.dot(spread, pair_grad, preferred_element_type=jnp.float32)
    symmetric = symmetric.astype(jnp.bfloat16).reshape(vectors, vectors, samples)
    gradients = jnp.einsum("fgb,bge->fbe", symmetric, features, preferred_element_type=jnp.float32)
    dense_grad = gradients[0]
    field_grads = gradients[1:].astype(jnp.bfloat16)
    fields = vectors - 1
    col_count = lax.axis_size("tab")
    rep_count = lax.axis_size("rep")
    capacity = 2 * samples // (col_count * rep_count)
    slot_total = col_count * rep_count * capacity
    ids_by_field = sample_ids.T

    def build_owner(pieces):
        column_ids, grads = pieces
        owners = column_ids // RQ
        slot_of = owners * capacity + arrival_order(owners, col_count * rep_count)
        return place_field(slot_of, column_ids % RQ, grads, slot_total)

    outgoing, row_tags = lax.map(build_owner, (ids_by_field, field_grads))
    outgoing = outgoing.reshape(fields, col_count, rep_count, capacity, depth)
    row_tags = row_tags.reshape(fields, col_count, rep_count, capacity)
    arrived, tags_in = (
        lax.all_to_all(
            lax.all_to_all(outgoing, "tab", split_axis=1, concat_axis=1, tiled=True),
            "rep",
            split_axis=2,
            concat_axis=2,
            tiled=True,
        ),
        lax.all_to_all(
            lax.all_to_all(row_tags, "tab", split_axis=1, concat_axis=1, tiled=True),
            "rep",
            split_axis=2,
            concat_axis=2,
            tiled=True,
        ),
    )
    table_grad = tally_rows(arrived.reshape(fields, -1, depth), tags_in.reshape(fields, -1), RQ)
    return (table_grad, dense_grad)


def solution(mesh):
    placed = (P(("tab", "rep"), None), P(("tab", "rep"), None, None), P(None, ("tab", "rep")))
    return jax.shard_map(
        local,
        mesh=mesh,
        in_specs=placed,
        out_specs=(P(None, ("tab", "rep"), None), P(("tab", "rep"), None)),
        check_vma=False,
    )
```

profile of v0, /device:TPU:0, one launch (start us, length us, event | category | flops | bytes accessed | tf_op | source)
XLA Modules:
  0.0 536.2 jit_solution(541020844716352694)
XLA Ops:
  0.7 2.7 convolution_convert_fusion
  3.4 2.2 reshape.112
  5.6 7.5 %copy.20 = bf16[27,27,512]{1,0,2:T(8,128)(2,1)} copy(bf16[27,27,512]{2,1,0:T(8,128)(2,1)} %reshape.112) | data formatting | bytes 1492992 | tf_op jit(solution)/shard_map/reshape | solution.py:52
  13.1 4.5 fusion.25
  18.8 2.1 copy-done.2
  22.2 173.3 %while.25 = (s32[]{:T(128)}, bf16[26,1024,128]{2,1,0:T(8,128)(2,1)}, s32[26,1024]{1,0:T(8,128)}, s32[26,512]{1,0:T(8,128)}, bf16[26,512,128]{2,1,0:T(8,128)(2,1)S(1)}, /*index=5*/s32[]{:T(128)}, s32[]{:T(128)}) while((s32[]{:T(128)}, bf16[26,1024,128]{2,1,0:T(8,128)(2,1)}, s32[26,1024]{1,0:T(8,128)}, s32[26,512]{1,0:T(8,128)}, ...), condition=%wide.region_4.5_spmd, body=%wide.region_0.4_spmd.sunk | while | flops 143897568 | bytes 717545 | solution.py:69
  39.7 1.4 dynamic_update_slice.26
  79.7 1.4 dynamic_update_slice.26
  86.4 1.4 dynamic_update_slice.26
  133.0 1.4 dynamic_update_slice.26
  139.7 1.4 dynamic_update_slice.26
  197.7 7.2 %all-to-all-start = ((s32[8,1,3328]{2,1,0:T(1,128)}), s32[8,1,3328]{2,1,0:T(1,128)S(1)}, u32[]{:S(2)}, u32[]{:S(2)}) async-start(s32[8,1,3328]{2,1,0:T(1,128)} %reshape.120), calls=%async_computation | async-start | bytes 212992 | tf_op jit(solution)/shard_map/all_to_all | solution.py:81
  205.0 8.6 %copy.26 = bf16[26,8,4,32,128]{4,3,2,0,1:T(8,128)(2,1)} copy(bf16[26,8,4,32,128]{4,3,2,1,0:T(8,128)(2,1)} %bitcast.88) | data formatting | bytes 13631488 | tf_op jit(solution)/shard_map/reshape | solution.py:70
  213.6 6.0 %all-to-all-start.2 = ((bf16[26,8,4,32,128]{4,3,2,0,1:T(8,128)(2,1)}), bf16[26,8,4,32,128]{4,3,2,0,1:T(8,128)(2,1)}, u32[]{:S(2)}, u32[]{:S(2)}) async-start(bf16[26,8,4,32,128]{4,3,2,0,1:T(8,128)(2,1)} %copy.26), calls=%async_computation.2 | async-start | bytes 13631488 | tf_op jit(solution)/shard_map/all_to_all | solution.py:74
  222.2 146.3 %all-to-all-done.2 = bf16[26,8,4,32,128]{4,3,2,0,1:T(8,128)(2,1)} async-done(((bf16[26,8,4,32,128]{4,3,2,0,1:T(8,128)(2,1)}), bf16[26,8,4,32,128]{4,3,2,0,1:T(8,128)(2,1)}, u32[]{:S(2)}, u32[]{:S(2)}) %all-to-all-start.2) | async-done | bytes 6815776 | tf_op jit(solution)/shard_map/all_to_all | solution.py:74
  368.5 3.5 all-to-all-start.1
  372.0 7.9 %copy.27 = bf16[26,8,4,32,128]{4,3,1,0,2:T(8,128)(2,1)} copy(bf16[26,8,4,32,128]{4,3,2,0,1:T(8,128)(2,1)} %all-to-all-done.2) | data formatting | bytes 13631488 | tf_op jit(solution)/shard_map/all_to_all | solution.py:74
  379.8 5.4 %all-to-all-start.3 = ((bf16[26,8,4,32,128]{4,3,1,0,2:T(8,128)(2,1)}), bf16[26,8,4,32,128]{4,3,1,0,2:T(8,128)(2,1)}, u32[]{:S(2)}, u32[]{:S(2)}) async-start(bf16[26,8,4,32,128]{4,3,1,0,2:T(8,128)(2,1)} %copy.27), calls=%async_computation.3 | async-start | bytes 13631488 | tf_op jit(solution)/shard_map/all_to_all | solution.py:73
  385.3 2.4 slice.25
  389.9 71.6 %all-to-all-done.3 = bf16[26,8,4,32,128]{4,3,1,0,2:T(8,128)(2,1)} async-done(((bf16[26,8,4,32,128]{4,3,1,0,2:T(8,128)(2,1)}), bf16[26,8,4,32,128]{4,3,1,0,2:T(8,128)(2,1)}, u32[]{:S(2)}, u32[]{:S(2)}) %all-to-all-start.3) | async-done | bytes 6815776 | tf_op jit(solution)/shard_map/all_to_all | solution.py:73
  461.6 8.0 %copy.28 = bf16[26,8,4,32,128]{4,3,2,1,0:T(8,128)(2,1)} copy(bf16[26,8,4,32,128]{4,3,1,0,2:T(8,128)(2,1)} %all-to-all-done.3) | data formatting | bytes 13631488 | tf_op jit(solution)/shard_map/all_to_all | solution.py:73
  469.6 66.7 %while.26 = (s32[]{:T(128)}, f32[26,128,128]{2,1,0:T(8,128)}, s32[26,1024]{1,0:T(8,128)}, bf16[26,1024,128]{2,1,0:T(8,128)(2,1)}, s32[]{:T(128)}) while((s32[]{:T(128)}, f32[26,128,128]{2,1,0:T(8,128)}, s32[26,1024]{1,0:T(8,128)}, bf16[26,1024,128]{2,1,0:T(8,128)(2,1)}, s32[]{:T(128)}) %tuple.59), condition=%wide.region_6.7_spmd, body=%wide.region_5.6_spmd.sunk | while | flops 33685504 | bytes 341065 | solution.py:43
  470.3 1.8 fusion.49
  472.9 1.8 fusion.49
  475.4 1.8 fusion.49
  478.0 1.8 fusion.49
  480.6 1.8 fusion.49
  483.1 1.8 fusion.49
  485.7 1.8 fusion.49
  488.3 1.8 fusion.49
  490.8 1.8 fusion.49
  493.4 1.8 fusion.49
  496.0 1.8 fusion.49
  498.5 1.8 fusion.49
  501.1 1.8 fusion.49
  503.7 1.8 fusion.49
  506.2 1.8 fusion.49
  508.8 1.8 fusion.49
  511.3 1.8 fusion.49
  513.9 1.8 fusion.49
  516.5 1.8 fusion.49
  519.0 1.8 fusion.49
  521.6 1.8 fusion.49
  524.2 1.8 fusion.49
  526.7 1.8 fusion.49
  529.3 1.8 fusion.49
  531.9 1.8 fusion.49
  534.4 1.8 fusion.49
  (435 shorter events, 194.9 us)
Async XLA Ops:
  0.6 12.5 %copy-start = (bf16[512,27,128]{2,0,1:T(8,128)(2,1)S(1)}, bf16[512,27,128]{2,0,1:T(8,128)(2,1)}, u32[]{:S(2)}) copy-start(bf16[512,27,128]{2,0,1:T(8,128)(2,1)} %param.9) | copy-start | bytes 10616836
  17.7 3.2 copy-start.2
  197.7 15.9 %all-to-all-start = ((s32[8,1,3328]{2,1,0:T(1,128)}), s32[8,1,3328]{2,1,0:T(1,128)S(1)}, u32[]{:S(2)}, u32[]{:S(2)}) async-start(s32[8,1,3328]{2,1,0:T(1,128)} %reshape.120), calls=%async_computation | async-start | bytes 212992 | tf_op jit(solution)/shard_map/all_to_all | solution.py:81
  213.6 154.9 %all-to-all-start.2 = ((bf16[26,8,4,32,128]{4,3,2,0,1:T(8,128)(2,1)}), bf16[26,8,4,32,128]{4,3,2,0,1:T(8,128)(2,1)}, u32[]{:S(2)}, u32[]{:S(2)}) async-start(bf16[26,8,4,32,128]{4,3,2,0,1:T(8,128)(2,1)} %copy.26), calls=%async_computation.2 | async-start | bytes 13631488 | tf_op jit(solution)/shard_map/all_to_all | solution.py:74
  368.5 11.4 %all-to-all-start.1 = ((s32[4,1,6656]{2,1,0:T(1,128)}), s32[4,1,6656]{2,1,0:T(1,128)S(1)}, u32[]{:S(2)}, u32[]{:S(2)}) async-start(s32[4,1,6656]{2,1,0:T(1,128)} %reshape.122), calls=%async_computation.1 | async-start | bytes 212992 | tf_op jit(solution)/shard_map/all_to_all | solution.py:80
  379.8 81.7 %all-to-all-start.3 = ((bf16[26,8,4,32,128]{4,3,1,0,2:T(8,128)(2,1)}), bf16[26,8,4,32,128]{4,3,1,0,2:T(8,128)(2,1)}, u32[]{:S(2)}, u32[]{:S(2)}) async-start(bf16[26,8,4,32,128]{4,3,1,0,2:T(8,128)(2,1)} %copy.27), calls=%async_computation.3 | async-start | bytes 13631488 | tf_op jit(solution)/shard_map/all_to_all | solution.py:73
  461.5 74.7 %copy-start.1 = (bf16[512,27,128]{2,0,1:T(8,128)(2,1)S(1)}, bf16[512,27,128]{2,0,1:T(8,128)(2,1)}, u32[]{:S(2)}) copy-start(bf16[512,27,128]{2,0,1:T(8,128)(2,1)} %param.9) | copy-start | bytes 10616836
where the time goes:
time: 544 us; the launch traced here: 536 us
  waiting for transfers between devices  218 us (40%)
  local copies, waits for them, and re-layouts  128 us (24%)
  matrix products  111 us (20%)
  other arithmetic  56.4 us (10%)
  starting transfers between devices  22.1 us (4%)
    all_to_all x1, waiting for transfers between devices, local(): lax.all_to_all(outgoing, 'tab', split_axis=1, concat_axis=1, tiled=True)  146 us
    all_to_all x1, waiting for transfers between devices, local(): lax.all_to_all(lax.all_to_all(outgoing, 'tab', split_axis=1, concat_axis=...  71.6 us
    dot_general x26, matrix products, per_field(): return jnp.dot(matches, slot_grads, preferred_element_type=jnp.float32)  46.8 us
    dynamic_update_slice x26, local copies, waits for them, and re-layouts, local(): outgoing, row_tags = lax.map(build_owner, (ids_by_field, field_grads))  36.6 us
    another operation x52, other arithmetic  31.3 us
    dot_general x26, matrix products, place_field(): jnp.dot(placing.astype(jnp.bfloat16), grads, preferred_element_type=jnp.f...  30.5 us
    dot_general x26, matrix products, place_field(): jnp.dot(placing.astype(jnp.float32), shifted, precision=lax.Precision.HIG...  26.3 us
    dynamic_slice x26, local copies, waits for them, and re-layouts, tally_rows(): return lax.map(per_field, (arrived, row_tags))  19.9 us
  transfers between devices with their start and end apart: 4, of which 2 were waited for; matrix products, arithmetic and copies ran while one was open for 4% of the time, Pallas kernels for 0%

commit v1 on v0

--- a/solution.py
+++ b/solution.py
@@ -44,6 +44,30 @@
 
 
 def local(sample_ids, features, pair_grad):
+
+    def rates_serve(vector, axis_name, which_dim, where_dim):
+        res, piece_next = (lax.axis_size(axis_name), lax.axis_index(axis_name))
+        parts_out = vector.shape[which_dim] // res
+        k_now = list(vector.shape)
+        k_now[which_dim] = parts_out
+        after = k_now[where_dim]
+        k_now[where_dim] = after * res
+        view_out = jnp.zeros(k_now, vector.dtype)
+        k0 = 0
+        while k0 < res:
+            current_block = lax.dynamic_slice_in_dim(
+                vector, (piece_next ^ k0) * parts_out, parts_out, axis=which_dim
+            )
+            if k0:
+                current_block = lax.ppermute(
+                    current_block, axis_name, [(src_i, src_i ^ k0) for src_i in range(res)]
+                )
+            view_out = lax.dynamic_update_slice_in_dim(
+                view_out, current_block, (piece_next ^ k0) * after, axis=where_dim
+            )
+            k0 += 1
+        return view_out
+
     vectors = features.shape[1]
     samples = features.shape[0]
     depth = features.shape[2]
@@ -71,11 +95,7 @@
     row_tags = row_tags.reshape(fields, col_count, rep_count, capacity)
     arrived, tags_in = (
         lax.all_to_all(
-            lax.all_to_all(outgoing, "tab", split_axis=1, concat_axis=1, tiled=True),
-            "rep",
-            split_axis=2,
-            concat_axis=2,
-            tiled=True,
+            rates_serve(outgoing, "tab", 1, 1), "rep", split_axis=2, concat_axis=2, tiled=True
         ),
         lax.all_to_all(
             lax.all_to_all(row_tags, "tab", split_axis=1, concat_axis=1, tiled=True),

time: 544 us -> 537 us (0.987)
  the two profiles are of different devices: /device:TPU:0 before, /device:TPU:8 now
where the time goes in v1:
time: 537 us; the launch traced here: 529 us
  waiting for transfers between devices  195 us (36%)
  local copies, waits for them, and re-layouts  137 us (26%)
  matrix products  111 us (21%)
  other arithmetic  56.5 us (11%)
  starting transfers between devices  28.5 us (5%)
    ppermute x7, waiting for transfers between devices, rates_serve(): lax.ppermute(current_block, axis_name, [(src_i, src_i ^ k0) for src_i in...  77.2 us
    all_to_all x1, waiting for transfers between devices, local(): lax.all_to_all(rates_serve(outgoing, 'tab', 1, 1), 'rep', split_axis=2, c...  69.6 us
    all_to_all x1, waiting for transfers between devices, local(): lax.all_to_all(row_tags, 'tab', split_axis=1, concat_axis=1, tiled=True)  48.3 us
    dot_general x26, matrix products, per_field(): return jnp.dot(matches, slot_grads, preferred_element_type=jnp.float32)  46.8 us
    dynamic_update_slice x26, local copies, waits for them, and re-layouts, local(): outgoing, row_tags = lax.map(build_owner, (ids_by_field, field_grads))  36.6 us
    another operation x52, other arithmetic  31.3 us
    dot_general x26, matrix products, place_field(): jnp.dot(placing.astype(jnp.bfloat16), grads, preferred_element_type=jnp.f...  30.3 us
    dot_general x26, matrix products, place_field(): jnp.dot(placing.astype(jnp.float32), shifted, precision=lax.Precision.HIG...  26.3 us
  transfers between devices with their start and end apart: 10, of which 5 were waited for; matrix products, arithmetic and copies ran while one was open for 6% of the time, Pallas kernels for 0%

profile of v1, /device:TPU:8, one launch (start us, length us, event | category | flops | bytes accessed | tf_op | source)
XLA Modules:
  0.0 529.1 jit_solution(14974358607876683724)
XLA Ops:
  0.7 2.7 convolution_convert_fusion
  3.4 2.2 reshape.112
  5.6 7.5 %copy.19 = bf16[27,27,512]{1,0,2:T(8,128)(2,1)} copy(bf16[27,27,512]{2,1,0:T(8,128)(2,1)} %reshape.112) | data formatting | bytes 1492992 | tf_op jit(solution)/shard_map/reshape | solution.py:76
  13.2 4.5 fusion.25
  20.9 173.2 %while.25 = (s32[]{:T(128)}, bf16[26,1024,128]{2,1,0:T(8,128)(2,1)}, s32[26,1024]{1,0:T(8,128)}, s32[26,512]{1,0:T(8,128)}, bf16[26,512,128]{2,1,0:T(8,128)(2,1)S(1)}, /*index=5*/s32[]{:T(128)}, s32[]{:T(128)}) while((s32[]{:T(128)}, bf16[26,1024,128]{2,1,0:T(8,128)(2,1)}, s32[26,1024]{1,0:T(8,128)}, s32[26,512]{1,0:T(8,128)}, ...), condition=%wide.region_4.5_spmd, body=%wide.region_0.4_spmd.sunk | while | flops 143897568 | bytes 717545 | solution.py:93
  194.1 6.7 %constant_dynamic-slice_fusion.2 = (bf16[26,1,4,32,128]{4,3,2,1,0:T(8,128)(2,1)S(1)}, bf16[26,1,4,32,128]{4,3,2,1,0:T(8,128)(2,1)S(1)}, bf16[26,1,4,32,128]{4,3,...) fusion(bf16[26,8,4,32,128]{4,3,2,1,0:T(8,128)(2,1)} %bitcast.87, ...), kind=kLoop, calls=%fused_computation.65 | loop fusion | bytes 13631520 | tf_op jit(solution)/shard_map/dynamic_slice | solution.py:58
  205.5 6.4 %all-to-all-start = ((s32[8,1,3328]{2,1,0:T(1,128)}), s32[8,1,3328]{2,1,0:T(1,128)S(1)}, u32[]{:S(2)}, u32[]{:S(2)}) async-start(s32[8,1,3328]{2,1,0:T(1,128)} %reshape.120), calls=%async_computation | async-start | bytes 212992 | tf_op jit(solution)/shard_map/all_to_all | solution.py:101
  211.9 2.4 collective-permute-start.6
  215.7 4.5 broadcast_in_dim.41
  221.4 48.3 %all-to-all-done = s32[8,1,3328]{2,1,0:T(1,128)S(1)} async-done(((s32[8,1,3328]{2,1,0:T(1,128)}), s32[8,1,3328]{2,1,0:T(1,128)S(1)}, u32[]{:S(2)}, u32[]{:S(2)}) %all-to-all-start) | async-done | bytes 106528 | tf_op jit(solution)/shard_map/all_to_all | solution.py:101
  272.4 3.3 all-to-all-start.1
  275.7 6.2 %collective-permute-start.4 = (bf16[26,1,4,32,128]{4,3,2,1,0:T(8,128)(2,1)S(1)}, bf16[26,1,4,32,128]{4,3,2,1,0:T(8,128)(2,1)S(1)}, u32[]{:S(2)}, u32[]{:S(2)}) collective-permute-start(bf16[26,1,4,32,128]{4,3,2,1,0:T(8,128)(2,1)S(1)} %copy-done.3), channel_id=1, source_target_pairs={{0,20},{4,16},{8,28},{12,24},{16,4},{20,0},{24,12},{28,8},{1,21},{... | collective-permute-start | bytes 2555912 | tf_op jit(solution)/shard_map/ppermute | solution.py:62
  281.9 2.3 copy_dynamic-update-slice_fusion.6
  284.2 2.3 copy_dynamic-update-slice_fusion.5
  286.5 2.2 copy_dynamic-update-slice_fusion.4
  288.7 45.0 %collective-permute-done.3 = bf16[26,1,4,32,128]{4,3,2,1,0:T(8,128)(2,1)} collective-permute-done((bf16[26,1,4,32,128]{4,3,2,1,0:T(8,128)(2,1)}, bf16[26,1,4,32,128]{4,3,2,1,0:T(8,128)(2,1)}, u32[]{:S(2)}, u32[]{:S(2)}) %collective-permute-start.3) | collective-permute-done | bytes 852000 | tf_op jit(solution)/shard_map/ppermute | solution.py:62
  333.7 2.3 copy_dynamic-update-slice_fusion.3
  336.0 15.8 %collective-permute-done.4 = bf16[26,1,4,32,128]{4,3,2,1,0:T(8,128)(2,1)S(1)} collective-permute-done((bf16[26,1,4,32,128]{4,3,2,1,0:T(8,128)(2,1)S(1)}, bf16[26,1,4,32,128]{4,3,2,1,0:T(8,128)(2,1)S(1)}, u32[]{:S(2)}, u32[]{:S(2)}) %collective-permute-start.4) | collective-permute-done | bytes 852000 | tf_op jit(solution)/shard_map/ppermute | solution.py:62
  353.0 16.4 %collective-permute-done.5 = bf16[26,1,4,32,128]{4,3,2,1,0:T(8,128)(2,1)S(1)} collective-permute-done((bf16[26,1,4,32,128]{4,3,2,1,0:T(8,128)(2,1)S(1)}, bf16[26,1,4,32,128]{4,3,2,1,0:T(8,128)(2,1)S(1)}, u32[]{:S(2)}, u32[]{:S(2)}) %collective-permute-start.5) | collective-permute-done | bytes 852000 | tf_op jit(solution)/shard_map/ppermute | solution.py:62
  370.6 2.3 copy_dynamic-update-slice_fusion
  372.9 5.3 %all-to-all-start.2 = ((bf16[26,8,4,32,128]{4,3,1,0,2:T(8,128)(2,1)}), bf16[26,8,4,32,128]{4,3,1,0,2:T(8,128)(2,1)}, u32[]{:S(2)}, u32[]{:S(2)}) async-start(bf16[26,8,4,32,128]{4,3,1,0,2:T(8,128)(2,1)} %copy_dynamic-update-slice_fusion), calls=%async_computation.2 | async-start | bytes 13631488 | tf_op jit(solution)/shard_map/all_to_all | solution.py:97
  378.2 2.4 slice.25
  382.7 2.1 reshape.114
  384.9 69.6 %all-to-all-done.2 = bf16[26,8,4,32,128]{4,3,1,0,2:T(8,128)(2,1)} async-done(((bf16[26,8,4,32,128]{4,3,1,0,2:T(8,128)(2,1)}), bf16[26,8,4,32,128]{4,3,1,0,2:T(8,128)(2,1)}, u32[]{:S(2)}, u32[]{:S(2)}) %all-to-all-start.2) | async-done | bytes 6815776 | tf_op jit(solution)/shard_map/all_to_all | solution.py:97
  454.5 7.9 %copy.33 = bf16[26,8,4,32,128]{4,3,2,1,0:T(8,128)(2,1)} copy(bf16[26,8,4,32,128]{4,3,1,0,2:T(8,128)(2,1)} %all-to-all-done.2) | data formatting | bytes 13631488 | tf_op jit(solution)/shard_map/all_to_all | solution.py:97
  462.4 66.7 %while.26 = (s32[]{:T(128)}, f32[26,128,128]{2,1,0:T(8,128)}, s32[26,1024]{1,0:T(8,128)}, bf16[26,1024,128]{2,1,0:T(8,128)(2,1)}, s32[]{:T(128)}) while((s32[]{:T(128)}, f32[26,128,128]{2,1,0:T(8,128)}, s32[26,1024]{1,0:T(8,128)}, bf16[26,1024,128]{2,1,0:T(8,128)(2,1)}, s32[]{:T(128)}) %tuple.66), condition=%wide.region_6.7_spmd, body=%wide.region_5.6_spmd.sunk | while | flops 33685504 | bytes 341065 | solution.py:43
  463.2 1.8 fusion.49
  465.7 1.8 fusion.49
  468.3 1.8 fusion.49
  470.8 1.8 fusion.49
  473.4 1.8 fusion.49
  476.0 1.8 fusion.49
  478.5 1.8 fusion.49
  481.1 1.8 fusion.49
  483.7 1.8 fusion.49
  486.2 1.8 fusion.49
  488.8 1.8 fusion.49
  491.4 1.8 fusion.49
  493.9 1.8 fusion.49
  496.5 1.8 fusion.49
  499.1 1.8 fusion.49
  501.6 1.8 fusion.49
  504.2 1.8 fusion.49
  506.7 1.8 fusion.49
  509.3 1.8 fusion.49
  514.4 1.8 fusion.49
  524.7 1.8 fusion.49
  527.3 1.8 fusion.49
  (459 shorter events, 217.2 us)
Async XLA Ops:
  0.6 12.5 %copy-start = (bf16[512,27,128]{2,0,1:T(8,128)(2,1)S(1)}, bf16[512,27,128]{2,0,1:T(8,128)(2,1)}, u32[]{:S(2)}) copy-start(bf16[512,27,128]{2,0,1:T(8,128)(2,1)} %param.9) | copy-start | bytes 10616836
  17.7 3.2 copy-start.2
  194.1 10.2 %copy-start.4 = (s32[26,1024]{1,0:T(8,128)S(1)}, s32[26,1024]{1,0:T(8,128)}, u32[]{:S(2)}) copy-start(s32[26,1024]{1,0:T(8,128)} %get-tuple-element.116) | copy-start | bytes 319492
  200.8 74.9 %collective-permute-start = (bf16[26,1,4,32,128]{4,3,2,1,0:T(8,128)(2,1)}, bf16[26,1,4,32,128]{4,3,2,1,0:T(8,128)(2,1)}, u32[]{:S(2)}, u32[]{:S(2)}) collective-permute-start(bf16[26,1,4,32,128]{4,3,2,1,0:T(8,128)(2,1)} %get-tuple-element.165), channel_id=1, source_target_pairs={{0,4},{4,0},{8,12},{12,8},{16,20},{20,16},{24,28},{28,24},{1,5},{5... | collective-permute-start | bytes 2555912 | tf_op jit(solution)/shard_map/ppermute | solution.py:62
  202.3 81.9 %collective-permute-start.1 = (bf16[26,1,4,32,128]{4,3,2,1,0:T(8,128)(2,1)}, bf16[26,1,4,32,128]{4,3,2,1,0:T(8,128)(2,1)}, u32[]{:S(2)}, u32[]{:S(2)}) collective-permute-start(bf16[26,1,4,32,128]{4,3,2,1,0:T(8,128)(2,1)} %get-tuple-element.164), channel_id=1, source_target_pairs={{0,8},{4,12},{8,0},{12,4},{16,24},{20,28},{24,16},{28,20},{1,9},{5... | collective-permute-start | bytes 2555912 | tf_op jit(solution)/shard_map/ppermute | solution.py:62
  202.8 83.7 %collective-permute-start.2 = (bf16[26,1,4,32,128]{4,3,2,1,0:T(8,128)(2,1)}, bf16[26,1,4,32,128]{4,3,2,1,0:T(8,128)(2,1)}, u32[]{:S(2)}, u32[]{:S(2)}) collective-permute-start(bf16[26,1,4,32,128]{4,3,2,1,0:T(8,128)(2,1)} %get-tuple-element.163), channel_id=1, source_target_pairs={{0,12},{4,8},{8,4},{12,0},{16,28},{20,24},{24,20},{28,16},{1,13},{... | collective-permute-start | bytes 2555912 | tf_op jit(solution)/shard_map/ppermute | solution.py:62
  205.5 70.2 %copy-start.3 = (bf16[26,1,4,32,128]{4,3,2,1,0:T(8,128)(2,1)S(1)}, bf16[26,1,4,32,128]{4,3,2,1,0:T(8,128)(2,1)}, u32[]{:S(2)}) copy-start(bf16[26,1,4,32,128]{4,3,2,1,0:T(8,128)(2,1)} %get-tuple-element.161) | copy-start | bytes 2555908
  205.5 64.1 %all-to-all-start = ((s32[8,1,3328]{2,1,0:T(1,128)}), s32[8,1,3328]{2,1,0:T(1,128)S(1)}, u32[]{:S(2)}, u32[]{:S(2)}) async-start(s32[8,1,3328]{2,1,0:T(1,128)} %reshape.120), calls=%async_computation | async-start | bytes 212992 | tf_op jit(solution)/shard_map/all_to_all | solution.py:101
  211.9 158.7 %collective-permute-start.6 = (bf16[26,1,4,32,128]{4,3,2,1,0:T(8,128)(2,1)S(1)}, bf16[26,1,4,32,128]{4,3,2,1,0:T(8,128)(2,1)}, u32[]{:S(2)}, u32[]{:S(2)}) collective-permute-start(bf16[26,1,4,32,128]{4,3,2,1,0:T(8,128)(2,1)S(1)} %get-tuple-element.159), channel_id=1, source_target_pairs={{0,28},{4,24},{8,20},{12,16},{16,12},{20,8},{24,4},{28,0},{1,29},{... | collective-permute-start | bytes 2555912 | tf_op jit(solution)/shard_map/ppermute | solution.py:62
  214.3 119.4 %collective-permute-start.3 = (bf16[26,1,4,32,128]{4,3,2,1,0:T(8,128)(2,1)}, bf16[26,1,4,32,128]{4,3,2,1,0:T(8,128)(2,1)}, u32[]{:S(2)}, u32[]{:S(2)}) collective-permute-start(bf16[26,1,4,32,128]{4,3,2,1,0:T(8,128)(2,1)} %get-tuple-element.162), channel_id=1, source_target_pairs={{0,16},{4,20},{8,24},{12,28},{16,0},{20,4},{24,8},{28,12},{1,17},{... | collective-permute-start | bytes 2555912 | tf_op jit(solution)/shard_map/ppermute | solution.py:62
  272.4 100.5 %all-to-all-start.1 = ((s32[4,1,6656]{2,1,0:T(1,128)}), s32[4,1,6656]{2,1,0:T(1,128)S(1)}, u32[]{:S(2)}, u32[]{:S(2)}) async-start(s32[4,1,6656]{2,1,0:T(1,128)} %reshape.122), calls=%async_computation.1 | async-start | bytes 212992 | tf_op jit(solution)/shard_map/all_to_all | solution.py:100
  275.7 76.1 %collective-permute-start.4 = (bf16[26,1,4,32,128]{4,3,2,1,0:T(8,128)(2,1)S(1)}, bf16[26,1,4,32,128]{4,3,2,1,0:T(8,128)(2,1)S(1)}, u32[]{:S(2)}, u32[]{:S(2)}) collective-permute-start(bf16[26,1,4,32,128]{4,3,2,1,0:T(8,128)(2,1)S(1)} %copy-done.3), channel_id=1, source_target_pairs={{0,20},{4,16},{8,28},{12,24},{16,4},{20,0},{24,12},{28,8},{1,21},{... | collective-permute-start | bytes 2555912 | tf_op jit(solution)/shard_map/ppermute | solution.py:62
  284.2 85.2 %collective-permute-start.5 = (bf16[26,1,4,32,128]{4,3,2,1,0:T(8,128)(2,1)S(1)}, bf16[26,1,4,32,128]{4,3,2,1,0:T(8,128)(2,1)S(1)}, u32[]{:S(2)}, u32[]{:S(2)}) collective-permute-start(bf16[26,1,4,32,128]{4,3,2,1,0:T(8,128)(2,1)S(1)} %get-tuple-element.160), channel_id=1, source_target_pairs={{0,24},{4,28},{8,16},{12,20},{16,8},{20,12},{24,0},{28,4},{1,25},{... | collective-permute-start | bytes 2555912 | tf_op jit(solution)/shard_map/ppermute | solution.py:62
  372.9 81.6 %all-to-all-start.2 = ((bf16[26,8,4,32,128]{4,3,1,0,2:T(8,128)(2,1)}), bf16[26,8,4,32,128]{4,3,1,0,2:T(8,128)(2,1)}, u32[]{:S(2)}, u32[]{:S(2)}) async-start(bf16[26,8,4,32,128]{4,3,1,0,2:T(8,128)(2,1)} %copy_dynamic-update-slice_fusion), calls=%async_computation.2 | async-start | bytes 13631488 | tf_op jit(solution)/shard_map/all_to_all | solution.py:97
  382.7 146.4 %copy-start.1 = (bf16[512,27,128]{2,0,1:T(8,128)(2,1)S(1)}, bf16[512,27,128]{2,0,1:T(8,128)(2,1)}, u32[]{:S(2)}) copy-start(bf16[512,27,128]{2,0,1:T(8,128)(2,1)} %param.9) | copy-start | bytes 10616836
